TPU v7x, 16 devices: a whole 2x2x2 slice. The times are simulated.
16 devices in a mesh: dp: 4 (over z, y), stage: 4 (over x, core).
Axes of the slice: x: 2, y: 2, z: 2, core: 2. Of those that a mesh axis runs over, the one named last changes fastest.
Arguments:
- token_ids: int32 [32, 256], P('dp'), parts along dimension 0
- label_ids: int32 [32, 256], P('dp'), parts along dimension 0
- embedding: bfloat16 [49152, 960], P('stage')
- w_in: bfloat16 [4, 960, 2560], P('stage')
- w_out: bfloat16 [4, 2560, 960], P('stage')
Outputs:
- output 1: float32 [4], P('dp'), parts along dimension 0
- output 2: float32 [16, 960, 2560], P(('dp', 'stage')), parts along dimension 0
- output 3: float32 [16, 2560, 960], P(('dp', 'stage')), parts along dimension 0
- output 4: float32 [196608, 960], P(('dp', 'stage')), parts along dimension 0
There are 4 independent parts. A program takes and returns all parts, laid end to end along the dimension named above; an argument that names none is the same for every part.
All inputs are finite; a program needn't handle non-finite values.
Results may differ from a plain program's by a relative error of at most 0.0110023.
Values are sent between devices in bfloat16 or wider.
A program may use at most 1 GiB of HBM per device.

v0:
```python
import jax
import jax.numpy as jnp
from jax import lax
from jax.sharding import PartitionSpec as P

NORM_EPS = 1e-6


def norm_f32(act_rows):
    acts_f = act_rows.astype(jnp.float32)
    return acts_f * lax.rsqrt(jnp.mean(acts_f * acts_f, axis=-1, keepdims=True) + NORM_EPS)


def layer_forward(act_rows, w_first, w_second):
    pre_act = jnp.dot(act_rows, w_first, preferred_element_type=jnp.float32)
    hidden = jax.nn.gelu(pre_act).astype(jnp.bfloat16)
    out_f = act_rows.astype(jnp.float32) + jnp.dot(hidden, w_second, preferred_element_type=jnp.float32)
    return out_f.astype(jnp.bfloat16)


def layer_backward(act_rows, grad_out, w_first, w_second):
    pre_act = jnp.dot(act_rows, w_first, preferred_element_type=jnp.float32)
    hidden_f, gelu_pull = jax.vjp(jax.nn.gelu, pre_act)
    hidden = hidden_f.astype(jnp.bfloat16)
    grad_second = jnp.einsum("tf,td->fd", hidden, grad_out, preferred_element_type=jnp.float32)
    grad_hidden = jnp.einsum("td,fd->tf", grad_out, w_second, preferred_element_type=jnp.float32)
    grad_pre = gelu_pull(grad_hidden)[0].astype(jnp.bfloat16)
    grad_first = jnp.einsum("td,tf->df", act_rows, grad_pre, preferred_element_type=jnp.float32)
    grad_in = (grad_out.astype(jnp.float32) + jnp.einsum("tf,df->td", grad_pre, w_first, preferred_element_type=jnp.float32)).astype(jnp.bfloat16)
    return grad_in, grad_first, grad_second


def take_slot(store_arr, mb_slot):
    return lax.dynamic_index_in_dim(store_arr, mb_slot, 0, keepdims=False)


def put_slot(store_arr, new_value, mb_slot, active):
    old_value = lax.dynamic_index_in_dim(store_arr, mb_slot, 0, keepdims=False)
    return lax.dynamic_update_index_in_dim(store_arr, jnp.where(active, new_value, old_value), mb_slot, 0)


def solution(mesh):
    n_stage = mesh.shape["stage"]
    fwd_pairs = [(src_idx, src_idx + 1) for src_idx in range(n_stage - 1)]
    bwd_pairs = [(src_idx + 1, src_idx) for src_idx in range(n_stage - 1)]

    def stage_body(token_ids, label_ids, emb_rows, w_in, w_out):
        stage_idx = lax.axis_index("stage")
        is_first = stage_idx == 0
        is_last = stage_idx == n_stage - 1
        micro_count, micro_tokens = token_ids.shape
        slice_rows, model_dim = emb_rows.shape
        logit_scale = model_dim ** -0.5
        w_first = w_in[0]
        w_second = w_out[0]
        n_ticks = micro_count + n_stage - 1
        row_start = stage_idx * slice_rows
        local_tok = token_ids - row_start
        tok_here = (local_tok >= 0) & (local_tok < slice_rows)
        looked_up = jnp.take(emb_rows, jnp.clip(local_tok, 0, slice_rows - 1), axis=0)
        embedded = lax.psum(jnp.where(tok_here[..., None], looked_up, 0), "stage")
        act_zeros = jnp.zeros((micro_tokens, model_dim), jnp.bfloat16)
        store_zeros = jnp.zeros((micro_count, micro_tokens, model_dim), jnp.bfloat16)

        def fwd_tick(tick_idx, loop_carry):
            incoming, saved_in, last_out = loop_carry
            micro_idx = tick_idx - stage_idx
            active = (micro_idx >= 0) & (micro_idx < micro_count)
            mb_slot = jnp.clip(micro_idx, 0, micro_count - 1)
            act_in = jnp.where(is_first, take_slot(embedded, mb_slot), incoming)
            act_out = lax.cond(active, lambda act_val: layer_forward(act_val, w_first, w_second), lambda act_val: act_val, act_in)
            saved_in = put_slot(saved_in, act_in, mb_slot, active)
            last_out = put_slot(last_out, act_out, mb_slot, active)
            return lax.ppermute(act_out, "stage", fwd_pairs), saved_in, last_out

        _, saved_in, last_out = lax.fori_loop(0, n_ticks, fwd_tick, (act_zeros, store_zeros, store_zeros))

        normed_f, norm_pull = jax.vjp(norm_f32, last_out)
        normed = lax.psum(jnp.where(is_last, normed_f.astype(jnp.bfloat16), 0), "stage")
        local_lab = label_ids - row_start
        vocab_iota = jnp.arange(slice_rows, dtype=jnp.int32)

        def head_step(loop_carry, inputs):
            grad_rows, loss_sum = loop_carry
            normed_mb, lab_mb = inputs
            logits = jnp.einsum("td,vd->tv", normed_mb, emb_rows, preferred_element_type=jnp.float32) * logit_scale
            row_max = lax.pmax(jnp.max(logits, axis=1), "stage")
            exp_logits = jnp.exp(logits - row_max[:, None])
            is_label = lab_mb[:, None] == vocab_iota[None, :]
            row_stats = lax.psum(jnp.stack([jnp.sum(exp_logits, axis=1), jnp.sum(jnp.where(is_label, logits, 0.0), axis=1)]), "stage")
            loss_sum = loss_sum + jnp.sum(jnp.log(row_stats[0]) + row_max - row_stats[1])
            grad_logits = ((exp_logits / row_stats[0][:, None] - is_label.astype(jnp.float32)) * logit_scale).astype(jnp.bfloat16)
            grad_n = lax.psum(jnp.einsum("tv,vd->td", grad_logits, emb_rows, preferred_element_type=jnp.float32), "stage")
            grad_rows = grad_rows + jnp.einsum("tv,td->vd", grad_logits, normed_mb, preferred_element_type=jnp.float32)
            return (grad_rows, loss_sum), grad_n

        head_init = (jnp.zeros((slice_rows, model_dim), jnp.float32), jnp.zeros((), jnp.float32))
        (grad_head, loss_sum), grad_norm = lax.scan(head_step, head_init, (normed, local_lab))
        grad_last = norm_pull(grad_norm)[0]

        def run_layer(operands):
            act_rows, grad_val, acc_a, acc_b = operands
            grad_in, grad_a, grad_b = layer_backward(act_rows, grad_val, w_first, w_second)
            return grad_in, acc_a + grad_a, acc_b + grad_b

        def skip_layer(operands):
            return operands[1], operands[2], operands[3]

        def bwd_tick(tick_idx, loop_carry):
            incoming, acc_first, acc_second, grad_embedded = loop_carry
            micro_idx = tick_idx - (n_stage - 1 - stage_idx)
            active = (micro_idx >= 0) & (micro_idx < micro_count)
            mb_slot = jnp.clip(micro_idx, 0, micro_count - 1)
            grad_out = jnp.where(is_last, take_slot(grad_last, mb_slot), incoming)
            grad_in, acc_first, acc_second = lax.cond(active, run_layer, skip_layer, (take_slot(saved_in, mb_slot), grad_out, acc_first, acc_second))
            grad_embedded = put_slot(grad_embedded, grad_in, mb_slot, active)
            return lax.ppermute(grad_in, "stage", bwd_pairs), acc_first, acc_second, grad_embedded

        bwd_init = (act_zeros, jnp.zeros(w_first.shape, jnp.float32), jnp.zeros(w_second.shape, jnp.float32), store_zeros)
        _, acc_first, acc_second, grad_embedded = lax.fori_loop(0, n_ticks, bwd_tick, bwd_init)

        grad_lookup_in = lax.psum(jnp.where(is_first, grad_embedded, 0), "stage")
        seg_ids = jnp.where(tok_here, local_tok, slice_rows).reshape(-1)
        grad_lookup = jax.ops.segment_sum(grad_lookup_in.reshape(-1, model_dim).astype(jnp.float32), seg_ids, num_segments=slice_rows)
        mean_loss = (loss_sum / (micro_count * micro_tokens)).reshape(1)
        return mean_loss, acc_first[None], acc_second[None], grad_head + grad_lookup

    return jax.shard_map(
        stage_body,
        mesh=mesh,
        in_specs=(P("dp", None), P("dp", None), P("stage", None), P("stage", None, None), P("stage", None, None)),
        out_specs=(P("dp"), P(("dp", "stage"), None, None), P(("dp", "stage"), None, None), P(("dp", "stage"), None)),
        check_vma=False,
    )
```

profile of v0, /device:TPU:0, one launch (start us, length us, event | category | flops | bytes accessed | tf_op | source)
XLA Modules:
  0.0 1740.9 jit_solution(2455743448534498367)
XLA Ops:
  9.3 32.0 %copy.22 = bf16[12288,960]{1,0:T(8,128)(2,1)} copy(bf16[12288,960]{0,1:T(8,128)(2,1)} %param.17) | data formatting | bytes 47185920 | tf_op args[2]
  41.3 22.3 %gather_fusion = bf16[2048,960]{1,0:T(8,128)(2,1)} fusion(bf16[12288,960]{1,0:T(8,128)(2,1)} %copy.22, s32[2048]{0:T(1024)S(1)} %broadcast_clamp_fusion), kind=kCustom, calls=%fused_computation | custom fusion | bytes 7872512 | tf_op jit(solution)/shard_map/jit(_take)/gather | solution.py:60
  82.9 71.9 %all-reduce.5.cloned.1.call-done = bf16[8,256,960]{1,2,0:T(8,128)(2,1)} async-done(((bf16[8,256,960]{1,2,0:T(8,128)(2,1)}), bf16[8,256,960]{1,2,0:T(8,128)(2,1)}) %all-reduce.5.cloned.1.call-update) | async-done | bytes 3932176 | tf_op jit(solution)/shard_map/psum | solution.py:61
  159.2 203.0 %while.53 = (s32[]{:T(128)}, bf16[256,960]{0,1:T(8,128)(2,1)S(1)}, bf16[8,256,960]{1,2,0:T(8,128)(2,1)}, bf16[8,256,960]{1,2,0:T(8,128)(2,1)}, s32[]{:T(128)}, /...) while((s32[]{:T(128)}, bf16[256,960]{0,1:T(8,128)(2,1)S(1)}, ...), condition=%wide.region_4.5_spmd, body=%wide.region_1.4_spmd.sunk | while | flops 2523955200 | bytes 19661588 | solution.py:76
  375.8 79.1 %all-reduce.7.cloned.1.call-done = bf16[8,256,960]{1,2,0:T(8,128)(2,1)} async-done(((bf16[8,256,960]{1,2,0:T(8,128)(2,1)}), bf16[8,256,960]{1,2,0:T(8,128)(2,1)}) %all-reduce.7.cloned.1.call-update) | async-done | bytes 3932176 | tf_op jit(solution)/shard_map/psum | solution.py:79
  454.8 722.9 %while.55 = (s32[]{:T(128)}, f32[12288,960]{0,1:T(8,128)}, f32[]{:T(128)}, f32[8,256,960]{1,2,0:T(8,128)}, bf16[8,256,960]{1,2,0:T(8,128)(2,1)}, /*index=5*/bf16...) while((s32[]{:T(128)}, f32[12288,960]{0,1:T(8,128)}, f32[]{:T(128)}, ...), condition=%wide.region_15.16_spmd.clone, body=%wide.region_7.15_spmd.clone.sunk | while | flops 18209292288 | bytes 201750736 | solution.py:98
  593.8 35.4 %select_add_fusion.2 = f32[12288,960]{0,1:T(8,128)} fusion(f32[12288,960]{0,1:T(8,128)} %get-tuple-element.937, pred[]{:T(512)S(6)} %compare.3, bf16[8,256,960]{1,2,0:T(8,128)(2,1)} %get-tuple-element.949, s32[]{:T(128)S(6)} %copy.66, f32[256,12288]{1,0:T(8,128)} %get-tuple-element.876, f32[256]{0:T(256)S(1)} %bitcast.120, s32[256]{0:T(256)S(1)} %bitcast.118, ...), kind=kOutput, calls=%fused_computation.63.clone.1 | convolution fusion | flops 6085410816 | bytes 107449352 | tf_op jit(solution)/shard_map/while/body/eval_jaxpr/tv,td->vd/dot_general | solution.py:94
  685.0 35.4 %select_add_fusion.2 = f32[12288,960]{0,1:T(8,128)} fusion(f32[12288,960]{0,1:T(8,128)} %get-tuple-element.937, pred[]{:T(512)S(6)} %compare.3, bf16[8,256,960]{1,2,0:T(8,128)(2,1)} %get-tuple-element.949, s32[]{:T(128)S(6)} %copy.66, f32[256,12288]{1,0:T(8,128)} %get-tuple-element.876, f32[256]{0:T(256)S(1)} %bitcast.120, s32[256]{0:T(256)S(1)} %bitcast.118, ...), kind=kOutput, calls=%fused_computation.63.clone.1 | convolution fusion | flops 6085410816 | bytes 107449352 | tf_op jit(solution)/shard_map/while/body/eval_jaxpr/tv,td->vd/dot_general | solution.py:94
  775.4 35.5 %select_add_fusion.2 = f32[12288,960]{0,1:T(8,128)} fusion(f32[12288,960]{0,1:T(8,128)} %get-tuple-element.937, pred[]{:T(512)S(6)} %compare.3, bf16[8,256,960]{1,2,0:T(8,128)(2,1)} %get-tuple-element.949, s32[]{:T(128)S(6)} %copy.66, f32[256,12288]{1,0:T(8,128)} %get-tuple-element.876, f32[256]{0:T(256)S(1)} %bitcast.120, s32[256]{0:T(256)S(1)} %bitcast.118, ...), kind=kOutput, calls=%fused_computation.63.clone.1 | convolution fusion | flops 6085410816 | bytes 107449352 | tf_op jit(solution)/shard_map/while/body/eval_jaxpr/tv,td->vd/dot_general | solution.py:94
  866.6 35.5 %select_add_fusion.2 = f32[12288,960]{0,1:T(8,128)} fusion(f32[12288,960]{0,1:T(8,128)} %get-tuple-element.937, pred[]{:T(512)S(6)} %compare.3, bf16[8,256,960]{1,2,0:T(8,128)(2,1)} %get-tuple-element.949, s32[]{:T(128)S(6)} %copy.66, f32[256,12288]{1,0:T(8,128)} %get-tuple-element.876, f32[256]{0:T(256)S(1)} %bitcast.120, s32[256]{0:T(256)S(1)} %bitcast.118, ...), kind=kOutput, calls=%fused_computation.63.clone.1 | convolution fusion | flops 6085410816 | bytes 107449352 | tf_op jit(solution)/shard_map/while/body/eval_jaxpr/tv,td->vd/dot_general | solution.py:94
  957.2 35.4 %select_add_fusion.2 = f32[12288,960]{0,1:T(8,128)} fusion(f32[12288,960]{0,1:T(8,128)} %get-tuple-element.937, pred[]{:T(512)S(6)} %compare.3, bf16[8,256,960]{1,2,0:T(8,128)(2,1)} %get-tuple-element.949, s32[]{:T(128)S(6)} %copy.66, f32[256,12288]{1,0:T(8,128)} %get-tuple-element.876, f32[256]{0:T(256)S(1)} %bitcast.120, s32[256]{0:T(256)S(1)} %bitcast.118, ...), kind=kOutput, calls=%fused_computation.63.clone.1 | convolution fusion | flops 6085410816 | bytes 107449352 | tf_op jit(solution)/shard_map/while/body/eval_jaxpr/tv,td->vd/dot_general | solution.py:94
  1048.3 35.4 %select_add_fusion.2 = f32[12288,960]{0,1:T(8,128)} fusion(f32[12288,960]{0,1:T(8,128)} %get-tuple-element.937, pred[]{:T(512)S(6)} %compare.3, bf16[8,256,960]{1,2,0:T(8,128)(2,1)} %get-tuple-element.949, s32[]{:T(128)S(6)} %copy.66, f32[256,12288]{1,0:T(8,128)} %get-tuple-element.876, f32[256]{0:T(256)S(1)} %bitcast.120, s32[256]{0:T(256)S(1)} %bitcast.118, ...), kind=kOutput, calls=%fused_computation.63.clone.1 | convolution fusion | flops 6085410816 | bytes 107449352 | tf_op jit(solution)/shard_map/while/body/eval_jaxpr/tv,td->vd/dot_general | solution.py:94
  1138.7 35.5 %select_add_fusion.2 = f32[12288,960]{0,1:T(8,128)} fusion(f32[12288,960]{0,1:T(8,128)} %get-tuple-element.937, pred[]{:T(512)S(6)} %compare.3, bf16[8,256,960]{1,2,0:T(8,128)(2,1)} %get-tuple-element.949, s32[]{:T(128)S(6)} %copy.66, f32[256,12288]{1,0:T(8,128)} %get-tuple-element.876, f32[256]{0:T(256)S(1)} %bitcast.120, s32[256]{0:T(256)S(1)} %bitcast.118, ...), kind=kOutput, calls=%fused_computation.63.clone.1 | convolution fusion | flops 6085410816 | bytes 107449352 | tf_op jit(solution)/shard_map/while/body/eval_jaxpr/tv,td->vd/dot_general | solution.py:94
  1201.4 343.7 %while.54 = (s32[]{:T(128)}, bf16[256,960]{0,1:T(8,128)(2,1)S(1)}, f32[960,2560]{1,0:T(8,128)}, f32[2560,960]{0,1:T(8,128)}, bf16[8,256,960]{1,2,0:T(8,128)(2,1)...) while((s32[]{:T(128)}, bf16[256,960]{0,1:T(8,128)(2,1)S(1)}, ...), condition=%wide.region_20.21_spmd, body=%wide.region_17.20_spmd.sunk | while | flops 6316605440 | bytes 234686576 | solution.py:120
  1221.3 64.1 %collective-permute-done.1 = bf16[256,960]{0,1:T(8,128)(2,1)S(1)} collective-permute-done((bf16[256,960]{0,1:T(8,128)(2,1)S(1)}, bf16[256,960]{0,1:T(8,128)(2,1)S(1)}, u32[]{:S(2)}, u32[]{:S(2)}) %collective-permute-start.1) | collective-permute-done | bytes 491552 | tf_op jit(solution)/shard_map/while/body/eval_jaxpr/ppermute | solution.py:117
  1286.5 22.0 %conditional.5 = (bf16[256,960]{0,1:T(8,128)(2,1)S(1)}, f32[960,2560]{1,0:T(8,128)}, f32[2560,960]{0,1:T(8,128)}) conditional(s32[]{:T(128)} %convert_element_type.124, (bf16[256,960]{0,1:T(8,128)(2,1)S(1)}, f32[960,2560]{1,0:T(8,128)}, f32[2560,960]{0,1:T(8,128)}) %tuple.121, (bf16[256,960]{0,1:T(8,128)(2,1)S(1)}, bf16[2560,960]{1,0:T(8,128)(2,1)}, ...), branch_computations={%region_18.18_spmd, %region_19.19_spmd} | conditional | flops 6316113920 | bytes 228787488 | solution.py:115
  1319.7 22.0 %conditional.5 = (bf16[256,960]{0,1:T(8,128)(2,1)S(1)}, f32[960,2560]{1,0:T(8,128)}, f32[2560,960]{0,1:T(8,128)}) conditional(s32[]{:T(128)} %convert_element_type.124, (bf16[256,960]{0,1:T(8,128)(2,1)S(1)}, f32[960,2560]{1,0:T(8,128)}, f32[2560,960]{0,1:T(8,128)}) %tuple.121, (bf16[256,960]{0,1:T(8,128)(2,1)S(1)}, bf16[2560,960]{1,0:T(8,128)(2,1)}, ...), branch_computations={%region_18.18_spmd, %region_19.19_spmd} | conditional | flops 6316113920 | bytes 228787488 | solution.py:115
  1353.0 22.0 %conditional.5 = (bf16[256,960]{0,1:T(8,128)(2,1)S(1)}, f32[960,2560]{1,0:T(8,128)}, f32[2560,960]{0,1:T(8,128)}) conditional(s32[]{:T(128)} %convert_element_type.124, (bf16[256,960]{0,1:T(8,128)(2,1)S(1)}, f32[960,2560]{1,0:T(8,128)}, f32[2560,960]{0,1:T(8,128)}) %tuple.121, (bf16[256,960]{0,1:T(8,128)(2,1)S(1)}, bf16[2560,960]{1,0:T(8,128)(2,1)}, ...), branch_computations={%region_18.18_spmd, %region_19.19_spmd} | conditional | flops 6316113920 | bytes 228787488 | solution.py:115
  1386.3 22.0 %conditional.5 = (bf16[256,960]{0,1:T(8,128)(2,1)S(1)}, f32[960,2560]{1,0:T(8,128)}, f32[2560,960]{0,1:T(8,128)}) conditional(s32[]{:T(128)} %convert_element_type.124, (bf16[256,960]{0,1:T(8,128)(2,1)S(1)}, f32[960,2560]{1,0:T(8,128)}, f32[2560,960]{0,1:T(8,128)}) %tuple.121, (bf16[256,960]{0,1:T(8,128)(2,1)S(1)}, bf16[2560,960]{1,0:T(8,128)(2,1)}, ...), branch_computations={%region_18.18_spmd, %region_19.19_spmd} | conditional | flops 6316113920 | bytes 228787488 | solution.py:115
  1419.5 22.0 %conditional.5 = (bf16[256,960]{0,1:T(8,128)(2,1)S(1)}, f32[960,2560]{1,0:T(8,128)}, f32[2560,960]{0,1:T(8,128)}) conditional(s32[]{:T(128)} %convert_element_type.124, (bf16[256,960]{0,1:T(8,128)(2,1)S(1)}, f32[960,2560]{1,0:T(8,128)}, f32[2560,960]{0,1:T(8,128)}) %tuple.121, (bf16[256,960]{0,1:T(8,128)(2,1)S(1)}, bf16[2560,960]{1,0:T(8,128)(2,1)}, ...), branch_computations={%region_18.18_spmd, %region_19.19_spmd} | conditional | flops 6316113920 | bytes 228787488 | solution.py:115
  1549.9 47.6 %copy.28 = f32[12288,960]{1,0:T(8,128)} copy(f32[12288,960]{0,1:T(8,128)} %get-tuple-element.537) | data formatting | bytes 94371840 | tf_op jit(solution)/shard_map/while | solution.py:98
  1597.6 29.8 %all-reduce.9.cloned.1.call-done = bf16[2048,960]{0,1:T(8,128)(2,1)} async-done(((bf16[2048,960]{0,1:T(8,128)(2,1)}), bf16[2048,960]{0,1:T(8,128)(2,1)}) %all-reduce.9.cloned.1.call-update) | async-done | bytes 3932176 | tf_op jit(solution)/shard_map/psum | solution.py:122
  1634.1 51.2 %scatter_fusion = f32[12288,960]{1,0:T(8,128)} fusion(f32[12288,960]{1,0:T(8,128)} %copy.28, s32[2048]{0:T(1024)S(1)} %bitcast.125, f32[2048,960]{1,0:T(8,128)} %copy.29), kind=kCustom, calls=%fused_computation.1 | custom fusion | flops 1966080 | bytes 23601152 | tf_op jit(solution)/shard_map/scatter-add | solution.py:124
  1685.3 47.5 %copy.30 = f32[12288,960]{0,1:T(8,128)} copy(f32[12288,960]{1,0:T(8,128)} %scatter_fusion) | data formatting | bytes 94371840
  (511 shorter events, 1149.5 us)
Async XLA Ops:
  7.2 147.6 %all-reduce.5.cloned.1.call-start = ((), (), s32[]{:S(2)}) async-start(), calls=%async_computation | async-start | bytes 7864320 | tf_op jit(solution)/shard_map/psum | solution.py:61
  74.5 380.3 %all-reduce.7.cloned.1.call-start = ((), (), s32[]{:S(2)}) async-start(), calls=%async_computation.1 | async-start | bytes 7864320 | tf_op jit(solution)/shard_map/psum | solution.py:79
  256.7 10.2 collective-permute-start
  277.2 10.1 collective-permute-start
  297.8 10.2 collective-permute-start
  311.0 17.5 %collective-permute-start = (bf16[256,960]{0,1:T(8,128)(2,1)S(1)}, bf16[256,960]{0,1:T(8,128)(2,1)S(1)}, u32[]{:S(2)}, u32[]{:S(2)}) collective-permute-start(bf16[256,960]{0,1:T(8,128)(2,1)S(1)} %get-tuple-element.999), channel_id=1, source_target_pairs={{0,1},{1,2},{2,3},{4,5},{5,6},{6,7},{8,9},{9,10},{10,11},{12,13},{... | collective-permute-start | bytes 1474568 | tf_op jit(solution)/shard_map/while/body/eval_jaxpr/ppermute | solution.py:74
  331.6 10.1 collective-permute-start
  344.8 17.5 %collective-permute-start = (bf16[256,960]{0,1:T(8,128)(2,1)S(1)}, bf16[256,960]{0,1:T(8,128)(2,1)S(1)}, u32[]{:S(2)}, u32[]{:S(2)}) collective-permute-start(bf16[256,960]{0,1:T(8,128)(2,1)S(1)} %get-tuple-element.999), channel_id=1, source_target_pairs={{0,1},{1,2},{2,3},{4,5},{5,6},{6,7},{8,9},{9,10},{10,11},{12,13},{... | collective-permute-start | bytes 1474568 | tf_op jit(solution)/shard_map/while/body/eval_jaxpr/ppermute | solution.py:74
  455.0 85.0 %all-reduce.11.cloned.1.call-start = ((), (), s32[]{:S(2)}) async-start(), calls=%async_computation.3 | async-start | bytes 1966080 | tf_op jit(solution)/shard_map/while/body/eval_jaxpr/psum | solution.py:93
  542.2 88.2 %all-reduce.11.cloned.1.call-start = ((), (), s32[]{:S(2)}) async-start(), calls=%async_computation.3 | async-start | bytes 1966080 | tf_op jit(solution)/shard_map/while/body/eval_jaxpr/psum | solution.py:93
  632.6 89.0 %all-reduce.11.cloned.1.call-start = ((), (), s32[]{:S(2)}) async-start(), calls=%async_computation.3 | async-start | bytes 1966080 | tf_op jit(solution)/shard_map/while/body/eval_jaxpr/psum | solution.py:93
  723.8 88.3 %all-reduce.11.cloned.1.call-start = ((), (), s32[]{:S(2)}) async-start(), calls=%async_computation.3 | async-start | bytes 1966080 | tf_op jit(solution)/shard_map/while/body/eval_jaxpr/psum | solution.py:93
  814.3 89.0 %all-reduce.11.cloned.1.call-start = ((), (), s32[]{:S(2)}) async-start(), calls=%async_computation.3 | async-start | bytes 1966080 | tf_op jit(solution)/shard_map/while/body/eval_jaxpr/psum | solution.py:93
  905.5 88.2 %all-reduce.11.cloned.1.call-start = ((), (), s32[]{:S(2)}) async-start(), calls=%async_computation.3 | async-start | bytes 1966080 | tf_op jit(solution)/shard_map/while/body/eval_jaxpr/psum | solution.py:93
  996.0 88.9 %all-reduce.11.cloned.1.call-start = ((), (), s32[]{:S(2)}) async-start(), calls=%async_computation.3 | async-start | bytes 1966080 | tf_op jit(solution)/shard_map/while/body/eval_jaxpr/psum | solution.py:93
  1087.1 88.2 %all-reduce.11.cloned.1.call-start = ((), (), s32[]{:S(2)}) async-start(), calls=%async_computation.3 | async-start | bytes 1966080 | tf_op jit(solution)/shard_map/while/body/eval_jaxpr/psum | solution.py:93
  1177.8 449.6 %all-reduce.9.cloned.1.call-start = ((), (), s32[]{:S(2)}) async-start(), calls=%async_computation.2 | async-start | bytes 7864320 | tf_op jit(solution)/shard_map/psum | solution.py:122
  1218.1 67.3 %collective-permute-start.1 = (bf16[256,960]{0,1:T(8,128)(2,1)S(1)}, bf16[256,960]{0,1:T(8,128)(2,1)S(1)}, u32[]{:S(2)}, u32[]{:S(2)}) collective-permute-start(bf16[256,960]{0,1:T(8,128)(2,1)S(1)} %get-tuple-element.866), channel_id=1, source_target_pairs={{1,0},{2,1},{3,2},{5,4},{6,5},{7,6},{9,8},{10,9},{11,10},{13,12},{... | collective-permute-start | bytes 1474568 | tf_op jit(solution)/shard_map/while/body/eval_jaxpr/ppermute | solution.py:117
  1308.5 10.1 collective-permute-start.1
  1341.8 10.1 collective-permute-start.1
  1375.0 10.1 collective-permute-start.1
  1408.3 10.1 collective-permute-start.1
  1441.6 10.1 collective-permute-start.1
  1474.8 10.1 collective-permute-start.1
  (89 other events, 388.3 us)
Sparse Core Ops, SparseCore 0:
  74.6 80.1 all-reduce.4
  369.5 85.3 all-reduce.6
  506.6 33.2 all-reduce.10
  593.9 33.1 all-reduce.10
  685.1 32.4 all-reduce.10
  775.5 33.0 all-reduce.10
  866.8 32.4 all-reduce.10
  957.3 33.0 all-reduce.10
  1048.4 32.4 all-reduce.10
  1138.8 33.1 all-reduce.10
  1550.0 77.2 all-reduce.8
where the time goes:
time: 1750 us; the launch traced here: 1740 us
  matrix products  730 us (42%)
  waiting for transfers between devices  311 us (18%)
  local copies, waits for them, and re-layouts  290 us (17%)
  other arithmetic  188 us (11%)
  starting transfers between devices  103 us (6%)
  blocking collectives  95.3 us (5%)
    dot_general x8, matrix products, head_step(): jnp.einsum('tv,td->vd', grad_logits, normed_mb, preferred_element_type=jn...  269 us
    dot_general x8, matrix products, head_step(): jnp.einsum('tv,vd->td', grad_logits, emb_rows, preferred_element_type=jnp...  152 us
    ppermute x11, waiting for transfers between devices, bwd_tick(): lax.ppermute(grad_in, 'stage', bwd_pairs)  119 us
    dot_general x8, matrix products, head_step(): jnp.einsum('td,vd->tv', normed_mb, emb_rows, preferred_element_type=jnp.f...  114 us
    unnamed x21, local copies, waits for them, and re-layouts  89.4 us
    ppermute x11, starting transfers between devices, fwd_tick(): return (lax.ppermute(act_out, 'stage', fwd_pairs), saved_in, last_out)  88.6 us
    psum x1, waiting for transfers between devices, stage_body(): lax.psum(jnp.where(is_last, normed_f.astype(jnp.bfloat16), 0), 'stage')  79.1 us
    psum x1, waiting for transfers between devices, stage_body(): embedded = lax.psum(jnp.where(tok_here[..., None], looked_up, 0), 'stage')  71.9 us
  transfers between devices with their start and end apart: 33, of which 15 were waited for; matrix products, arithmetic and copies ran while one was open for 22% of the time, Pallas kernels for 0%

commit v1 on v0

v1 whole, which is shorter than its diff:
```python
import functools

import jax
import jax.numpy as jnp
from jax import lax
from jax.experimental import pallas as pl
from jax.experimental.pallas import tpu as pltpu
from jax.sharding import PartitionSpec as P

NORM_EPS = 1e-6
GELU_A = 0.7978845608028654
GELU_B = 0.044715
NN = (((1,), (0,)), ((), ()))
NT = (((1,), (1,)), ((), ()))
TN = (((0,), (0,)), ((), ()))
MESH = pl.DeviceIdType.MESH
BF16 = jnp.bfloat16
F32 = jnp.float32
VMEM_ALL = 66_000_000
CHUNK = 256
LOOK_TILE = 512
HEAD_ROWS = 512
HEAD_TILE = 1024
FFN_TILE = 512


def mm(lhs, rhs, dims=NN):
    return lax.dot_general(lhs, rhs, dims, preferred_element_type=F32)


def one_hot(match):
    return jnp.where(match, 1.0, 0.0).astype(BF16)


def params(n_axes=0, **kwargs):
    if n_axes:
        kwargs["dimension_semantics"] = ("arbitrary",) * n_axes
    kwargs.setdefault("vmem_limit_bytes", VMEM_ALL)
    return pltpu.CompilerParams(**kwargs)


def vmem():
    return pl.BlockSpec(memory_space=pltpu.VMEM)


def chunk_bounds(starts, tile_idx):
    lo, hi = starts[tile_idx], starts[tile_idx + 1]
    first = lo // CHUNK
    return first, jnp.where(hi > lo, (hi + CHUNK - 1) // CHUNK, first)


def lookup_kernel(starts, ids_ref, rank_ref, table_ref, out_ref, acc, packed):
    tile_idx = pl.program_id(0)
    n_tiles = pl.num_programs(0)
    n_chunk = acc.shape[0]

    @pl.when(tile_idx == 0)
    def _():
        acc[...] = jnp.zeros_like(acc)

    first, last = chunk_bounds(starts, tile_idx)
    base = starts[n_tiles + 1] + tile_idx * LOOK_TILE

    def step(c, _):
        rows = lax.broadcasted_iota(jnp.int32, (LOOK_TILE, CHUNK), 0) + base
        acc[c] += mm(table_ref[...], one_hot(rows == ids_ref[c]))
        return 0

    lax.fori_loop(first, last, step, 0)

    @pl.when(tile_idx == n_tiles - 1)
    def _():
        packed[...] = acc[...].astype(BF16)

        def back(m, _):
            slot = lax.broadcasted_iota(jnp.int32, (rank_ref.shape[1], CHUNK), 1)
            total = mm(one_hot(slot == rank_ref[m]), packed[0], NT)
            for c in range(1, n_chunk):
                total += mm(one_hot(slot + c * CHUNK == rank_ref[m]), packed[c], NT)
            out_ref[m] = total.astype(BF16)
            return 0

        lax.fori_loop(0, out_ref.shape[0], back, 0)


def run_lookup(starts, ids_rows, rank_cols, table_t):
    dim, rows = table_t.shape
    n_micro, tokens = rank_cols.shape[:2]
    n_chunk = n_micro * tokens // CHUNK
    whole = lambda *shape: pl.BlockSpec(shape, lambda i, s: (0,) * len(shape))
    return pl.pallas_call(
        lookup_kernel,
        out_shape=jax.ShapeDtypeStruct((n_micro, tokens, dim), BF16),
        grid_spec=pltpu.PrefetchScalarGridSpec(
            num_scalar_prefetch=1,
            grid=(rows // LOOK_TILE,),
            in_specs=[whole(n_chunk, 1, CHUNK), whole(n_micro, tokens, 1), pl.BlockSpec((dim, LOOK_TILE), lambda i, s: (0, i))],
            out_specs=whole(n_micro, tokens, dim),
            scratch_shapes=[pltpu.VMEM((n_chunk, dim, CHUNK), F32), pltpu.VMEM((n_chunk, dim, CHUNK), BF16)],
        ),
        compiler_params=params(1),
        name="lookup",
    )(starts, ids_rows, rank_cols, table_t)


def peer_copy(src, dst, send, recv, slot, group, stage):
    return pltpu.make_async_remote_copy(
        src_ref=src.at[slot], dst_ref=dst.at[slot], send_sem=send.at[slot], recv_sem=recv.at[slot],
        device_id=(group, stage), device_id_type=MESH)


def greet(group, stage, n_stage):
    barrier = pltpu.get_barrier_semaphore()
    for off in range(1, n_stage):
        pl.semaphore_signal(barrier, inc=1, device_id=(group, lax.rem(stage + off, n_stage)), device_id_type=MESH)
    pl.semaphore_wait(barrier, n_stage - 1)


def each(count, body):
    def step(m, _):
        body(m)
        return 0

    lax.fori_loop(0, count, step, 0)


def gelu_parts(pre):
    inner = jnp.tanh(GELU_A * (pre + GELU_B * pre * pre * pre))
    return inner


def fwd_kernel(part, w1, w2, saved, last, near, far, outbox, acc,
               near_s, near_r, far_s, far_r, act_s, act_r, top_s, top2_s, top_r):
    group, stage = lax.axis_index("dp"), lax.axis_index("stage")
    count = part.shape[0]
    ffn = w1.shape[1]
    greet(group, stage, 4)

    def near_copy(m):
        return peer_copy(part, near, near_s, near_r, m, group, jnp.maximum(stage - 1, 0))

    def far_copy(m):
        return peer_copy(far, far, far_s, far_r, m, group, 0)

    def act_copy(m):
        return peer_copy(outbox, saved, act_s, act_r, m, group, jnp.minimum(stage + 1, 3))

    def top_copy(m, target, sem):
        return peer_copy(last, last, sem, top_r, m, group, target)

    odd = lax.rem(stage, 2) == 1

    @pl.when(odd)
    def _():
        each(count, lambda m: near_copy(m).start())

    @pl.when(stage == 2)
    def _():
        def body(m):
            near_copy(m).wait_recv()
            far[m] = part[m] + near[m]
            far_copy(m).start()

        each(count, body)

    def layer(m):
        @pl.when(stage == 0)
        def _():
            near_copy(m).wait_recv()
            pltpu.make_async_remote_copy(
                src_ref=far.at[m], dst_ref=far.at[m], send_sem=far_s.at[m], recv_sem=far_r.at[m],
                device_id=(group, 2), device_id_type=MESH).wait_recv()
            saved[m] = part[m] + near[m] + far[m]

        @pl.when(stage > 0)
        def _():
            pltpu.make_async_remote_copy(
                src_ref=outbox.at[m], dst_ref=saved.at[m], send_sem=act_s.at[m], recv_sem=act_r.at[m],
                device_id=(group, jnp.maximum(stage - 1, 0)), device_id_type=MESH).wait_recv()

        acts = saved[m]
        for j in range(ffn // FFN_TILE):
            cols = pl.ds(j * FFN_TILE, FFN_TILE)
            pre = mm(acts, w1[:, cols])
            hidden = (0.5 * pre * (1.0 + gelu_parts(pre))).astype(BF16)
            prod = mm(hidden, w2[:, cols], NT)
            if j == 0:
                acc[...] = prod
            else:
                acc[...] += prod
        result = (acts.astype(F32) + acc[...]).astype(BF16)

        @pl.when(stage < 3)
        def _():
            outbox[m] = result
            act_copy(m).start()

        @pl.when(stage == 3)
        def _():
            last[m] = result
            top_copy(m, 1, top_s).start()
            top_copy(m, 2, top2_s).start()

    each(count, layer)

    @pl.when(stage == 1)
    def _():
        def body(m):
            top_copy(m, 0, top_s).wait_recv()
            top_copy(m, 0, top_s).start()

        each(count, body)
        each(count, lambda m: top_copy(m, 0, top_s).wait_send())

    @pl.when(lax.rem(stage, 2) == 0)
    def _():
        each(count, lambda m: top_copy(m, 3, top_s).wait_recv())

    @pl.when(odd)
    def _():
        each(count, lambda m: near_copy(m).wait_send())

    @pl.when(stage == 2)
    def _():
        each(count, lambda m: far_copy(m).wait_send())

    @pl.when(stage < 3)
    def _():
        each(count, lambda m: act_copy(m).wait_send())

    @pl.when(stage == 3)
    def _():
        def body(m):
            top_copy(m, 1, top_s).wait_send()
            top_copy(m, 2, top2_s).wait_send()

        each(count, body)


def run_forward(part, w1, w2):
    count = part.shape[0]
    shape = part.shape
    return pl.pallas_call(
        fwd_kernel,
        out_shape=(jax.ShapeDtypeStruct(shape, BF16), jax.ShapeDtypeStruct(shape, BF16)),
        in_specs=[vmem()] * 3,
        out_specs=(vmem(), vmem()),
        scratch_shapes=[pltpu.VMEM(shape, BF16)] * 3 + [pltpu.VMEM(shape[1:], F32)] + [pltpu.SemaphoreType.DMA((count,))] * 9,
        compiler_params=params(collective_id=0, has_side_effects=True),
        name="forward",
    )(part, w1, w2)


def head_kernel(scale, x_ref, lab_ref, table_ref, prob_ref, norm_ref, max_ref, sum_ref, pick_ref):
    tile_idx = pl.program_id(1)

    @pl.when(tile_idx == 0)
    def _():
        acts = x_ref[...].astype(F32)
        norm_ref[...] = (acts * lax.rsqrt(jnp.mean(acts * acts, axis=-1, keepdims=True) + NORM_EPS)).astype(BF16)
        max_ref[...] = jnp.full(max_ref.shape, jnp.finfo(F32).min, F32)
        sum_ref[...] = jnp.zeros(sum_ref.shape, F32)
        pick_ref[...] = jnp.zeros(pick_ref.shape, F32)

    logits = mm(norm_ref[...], table_ref[...]) * scale
    top = jnp.max(logits, axis=1, keepdims=True)
    prob = jnp.exp(logits - top)
    prob_ref[...] = prob.astype(BF16)
    cols = lax.broadcasted_iota(jnp.int32, logits.shape, 1) + tile_idx * HEAD_TILE
    picked = jnp.sum(jnp.where(cols == lab_ref[...], logits, 0.0), axis=1, keepdims=True)
    here = lax.broadcasted_iota(jnp.int32, max_ref.shape, 1) == tile_idx
    max_ref[...] = jnp.where(here, top, max_ref[...])
    sum_ref[...] = jnp.where(here, jnp.sum(prob, axis=1, keepdims=True), sum_ref[...])
    pick_ref[...] = jnp.where(here, picked, pick_ref[...])


def run_head(acts, labels, table_t, scale):
    tokens, dim = acts.shape
    rows = table_t.shape[1]
    stat = pl.BlockSpec((HEAD_ROWS, 128), lambda i, j: (i, 0))
    return pl.pallas_call(
        functools.partial(head_kernel, scale),
        out_shape=(jax.ShapeDtypeStruct((tokens, rows), BF16), jax.ShapeDtypeStruct((tokens, dim), BF16)) + (jax.ShapeDtypeStruct((tokens, 128), F32),) * 3,
        grid=(tokens // HEAD_ROWS, rows // HEAD_TILE),
        in_specs=[pl.BlockSpec((HEAD_ROWS, dim), lambda i, j: (i, 0)), pl.BlockSpec((HEAD_ROWS, 1), lambda i, j: (i, 0)), pl.BlockSpec((dim, HEAD_TILE), lambda i, j: (0, j))],
        out_specs=(pl.BlockSpec((HEAD_ROWS, HEAD_TILE), lambda i, j: (i, j)), pl.BlockSpec((HEAD_ROWS, dim), lambda i, j: (i, 0)), stat, stat, stat),
        compiler_params=params(2),
        name="head",
    )(acts, labels, table_t)


def head_grad_kernel(prob_ref, coef_ref, lab_ref, lab_coef_ref, table_ref, grad_ref, out_ref, acc):
    tile_idx = pl.program_id(1)
    here = lax.broadcasted_iota(jnp.int32, coef_ref.shape, 1) == tile_idx
    coef = jnp.sum(jnp.where(here, coef_ref[...], 0.0), axis=1, keepdims=True)
    cols = lax.broadcasted_iota(jnp.int32, prob_ref.shape, 1) + tile_idx * HEAD_TILE
    grad = jnp.where(cols == lab_ref[...], lab_coef_ref[...], prob_ref[...].astype(F32) * coef).astype(BF16)
    grad_ref[...] = grad
    prod = mm(grad, table_ref[...], NT)

    @pl.when(tile_idx == 0)
    def _():
        acc[...] = prod

    @pl.when(tile_idx > 0)
    def _():
        acc[...] += prod

    @pl.when(tile_idx == pl.num_programs(1) - 1)
    def _():
        out_ref[...] = acc[...]


def run_head_grad(prob, coef, labels, lab_coef, table_t):
    tokens, rows = prob.shape
    dim = table_t.shape[0]
    tile = pl.BlockSpec((HEAD_ROWS, HEAD_TILE), lambda i, j: (i, j))
    col = pl.BlockSpec((HEAD_ROWS, 1), lambda i, j: (i, 0))
    return pl.pallas_call(
        head_grad_kernel,
        out_shape=(jax.ShapeDtypeStruct((tokens, rows), BF16), jax.ShapeDtypeStruct((tokens, dim), F32)),
        grid=(tokens // HEAD_ROWS, rows // HEAD_TILE),
        in_specs=[tile, pl.BlockSpec((HEAD_ROWS, 128), lambda i, j: (i, 0)), col, col, pl.BlockSpec((dim, HEAD_TILE), lambda i, j: (0, j))],
        out_specs=(tile, pl.BlockSpec((HEAD_ROWS, dim), lambda i, j: (i, 0))),
        scratch_shapes=[pltpu.VMEM((HEAD_ROWS, dim), F32)],
        compiler_params=params(2),
        name="head_grad",
    )(prob, coef, labels, lab_coef, table_t)


def bwd_kernel(gn, last, saved, w1, w2, dy, gx, hid_out, pre_out,
               near, far, outbox, own, hid, dpre, acc,
               near_s, near_r, far_s, far_r, act_s, act_r, low_s, low2_s, low_r, own_sem, hid_sem, pre_sem):
    group, stage = lax.axis_index("dp"), lax.axis_index("stage")
    count = last.shape[0]
    ffn = w1.shape[1]
    greet(group, stage, 4)
    even = lax.rem(stage, 2) == 0

    def near_copy(m):
        return peer_copy(gn, near, near_s, near_r, m, group, jnp.where(even, stage + 1, stage - 1))

    def far_copy(m, target):
        return peer_copy(far, far, far_s, far_r, m, group, target)

    def act_copy(m, target):
        return peer_copy(outbox, dy, act_s, act_r, m, group, target)

    def low_copy(m, target, sem):
        return peer_copy(gx, gx, sem, low_r, m, group, target)

    def own_copy(m):
        return pltpu.make_async_copy(gn.at[m], own.at[lax.rem(m, 2)], own_sem.at[lax.rem(m, 2)])

    def hid_copy(m):
        return pltpu.make_async_copy(hid.at[lax.rem(m, 2)], hid_out.at[m], hid_sem.at[lax.rem(m, 2)])

    def pre_copy(m):
        return pltpu.make_async_copy(dpre.at[lax.rem(m, 2)], pre_out.at[m], pre_sem.at[lax.rem(m, 2)])

    @pl.when(even)
    def _():
        each(count, lambda m: near_copy(m).start())

    @pl.when(jnp.logical_not(even))
    def _():
        own_copy(0).start()

    def next_own(m):
        @pl.when(m + 1 < count)
        def _():
            own_copy(m + 1).start()

        own_copy(m).wait()
        near_copy(m).wait_recv()

    @pl.when(stage == 1)
    def _():
        def body(m):
            next_own(m)
            far[m] = (own[lax.rem(m, 2)] + near[m]).astype(BF16)
            far_copy(m, 3).start()

        each(count, body)

    def layer(m):
        slot = lax.rem(m, 2)

        @pl.when(stage == 3)
        def _():
            next_own(m)
            far_copy(m, 1).wait_recv()
            grad_n = own[slot] + near[m] + far[m].astype(F32)
            acts = last[m].astype(F32)
            inv = lax.rsqrt(jnp.mean(acts * acts, axis=-1, keepdims=True) + NORM_EPS)
            inner = jnp.mean(acts * grad_n, axis=-1, keepdims=True)
            dy[m] = (inv * (grad_n - acts * (inv * inv * inner))).astype(BF16)

        @pl.when(stage < 3)
        def _():
            act_copy(m, jnp.minimum(stage + 1, 3)).wait_recv()

        @pl.when(m >= 2)
        def _():
            hid_copy(m - 2).wait()
            pre_copy(m - 2).wait()

        acts = saved[m]
        grad = dy[m]
        for j in range(ffn // FFN_TILE):
            cols = pl.ds(j * FFN_TILE, FFN_TILE)
            pre = mm(acts, w1[:, cols])
            th = gelu_parts(pre)
            half = 0.5 * (1.0 + th)
            hid[slot, :, cols] = (pre * half).astype(BF16)
            slope = half + 0.5 * pre * (1.0 - th * th) * (GELU_A * (1.0 + 3.0 * GELU_B * pre * pre))
            down = (mm(grad, w2[:, cols]) * slope).astype(BF16)
            dpre[slot, :, cols] = down
            prod = mm(down, w1[:, cols], NT)
            if j == 0:
                acc[...] = prod
            else:
                acc[...] += prod
        result = (grad.astype(F32) + acc[...]).astype(BF16)
        hid_copy(m).start()
        pre_copy(m).start()

        @pl.when(stage > 0)
        def _():
            outbox[m] = result
            act_copy(m, jnp.maximum(stage - 1, 0)).start()

        @pl.when(stage == 0)
        def _():
            gx[m] = result
            low_copy(m, 1, low_s).start()
            low_copy(m, 2, low2_s).start()

    each(count, layer)

    @pl.when(stage == 2)
    def _():
        def body(m):
            low_copy(m, 3, low_s).wait_recv()
            low_copy(m, 3, low_s).start()

        each(count, body)
        each(count, lambda m: low_copy(m, 3, low_s).wait_send())

    @pl.when(jnp.logical_not(even))
    def _():
        each(count, lambda m: low_copy(m, 0, low_s).wait_recv())

    @pl.when(even)
    def _():
        each(count, lambda m: near_copy(m).wait_send())

    @pl.when(stage == 1)
    def _():
        each(count, lambda m: far_copy(m, 3).wait_send())

    @pl.when(stage > 0)
    def _():
        each(count, lambda m: act_copy(m, jnp.maximum(stage - 1, 0)).wait_send())

    @pl.when(stage == 0)
    def _():
        def body(m):
            low_copy(m, 1, low_s).wait_send()
            low_copy(m, 2, low2_s).wait_send()

        each(count, body)

    for m in range(count - 2, count):
        hid_copy(m).wait()
        pre_copy(m).wait()


def run_backward(gn, last, saved, w1, w2):
    shape = saved.shape
    count, tokens, dim = shape
    ffn = w1.shape[1]
    any_spec = pl.BlockSpec(memory_space=pl.ANY)
    wide = jax.ShapeDtypeStruct((count, tokens, ffn), BF16)
    return pl.pallas_call(
        bwd_kernel,
        out_shape=(jax.ShapeDtypeStruct(shape, BF16), jax.ShapeDtypeStruct(shape, BF16), wide, wide),
        in_specs=[any_spec] + [vmem()] * 4,
        out_specs=(vmem(), vmem(), any_spec, any_spec),
        scratch_shapes=[
            pltpu.VMEM(shape, F32), pltpu.VMEM(shape, BF16), pltpu.VMEM(shape, BF16), pltpu.VMEM((2, tokens, dim), F32),
            pltpu.VMEM((2, tokens, ffn), BF16), pltpu.VMEM((2, tokens, ffn), BF16), pltpu.VMEM((tokens, dim), F32),
        ] + [pltpu.SemaphoreType.DMA((count,))] * 9 + [pltpu.SemaphoreType.DMA((2,))] * 3,
        compiler_params=params(collective_id=1, has_side_effects=True),
        name="backward",
    )(gn, last, saved, w1, w2)


def weight_kernel(x_ref, dpre_ref, dy_ref, hid_ref, first_ref, second_ref, xt, dyt):
    @pl.when(pl.program_id(0) == 0)
    def _():
        xt[...] = x_ref[...].T
        dyt[...] = dy_ref[...].T

    first_ref[...] = mm(xt[...], dpre_ref[...])
    second_ref[...] = mm(dyt[...], hid_ref[...])


def run_weights(acts, dpre, dy, hid):
    tokens, dim = acts.shape
    ffn = hid.shape[1]
    whole = pl.BlockSpec((tokens, dim), lambda j: (0, 0))
    tile = pl.BlockSpec((tokens, FFN_TILE), lambda j: (0, j))
    out = pl.BlockSpec((dim, FFN_TILE), lambda j: (0, j))
    return pl.pallas_call(
        weight_kernel,
        out_shape=(jax.ShapeDtypeStruct((dim, ffn), F32),) * 2,
        grid=(ffn // FFN_TILE,),
        in_specs=[whole, tile, whole, tile],
        out_specs=(out, out),
        scratch_shapes=[pltpu.VMEM((dim, tokens), BF16)] * 2,
        compiler_params=params(1),
        name="weights",
    )(acts, dpre, dy, hid)


def table_kernel(starts, ids_ref, rank_ref, norm_ref, gx_ref, grad_ref, out_ref, normt, packed):
    tile_idx = pl.program_id(0)
    n_tiles = pl.num_programs(0)
    n_chunk = packed.shape[0]
    n_micro = gx_ref.shape[0]

    @pl.when(tile_idx == 0)
    def _():
        normt[...] = norm_ref[...].T
        slot = lax.broadcasted_iota(jnp.int32, (rank_ref.shape[1], CHUNK), 1)

        def gather(c, _):
            total = mm(gx_ref[0], one_hot(slot + c * CHUNK == rank_ref[0]), TN)
            for m in range(1, n_micro):
                total += mm(gx_ref[m], one_hot(slot + c * CHUNK == rank_ref[m]), TN)
            packed[c] = total.astype(BF16)
            return 0

        lax.fori_loop(0, n_chunk, gather, 0)

    out_ref[...] = mm(normt[...], grad_ref[...])
    first, last = chunk_bounds(starts, tile_idx)
    base = starts[n_tiles + 1] + tile_idx * LOOK_TILE

    def step(c, _):
        rows = lax.broadcasted_iota(jnp.int32, (CHUNK, LOOK_TILE), 1) + base
        out_ref[...] += mm(packed[c], one_hot(rows == ids_ref[c]))
        return 0

    lax.fori_loop(first, last, step, 0)


def run_table(starts, ids_cols, rank_cols, normed, gx, grad):
    tokens, rows = grad.shape
    n_micro, micro, dim = gx.shape
    n_chunk = tokens // CHUNK
    whole = lambda *shape: pl.BlockSpec(shape, lambda i, s: (0,) * len(shape))
    return pl.pallas_call(
        table_kernel,
        out_shape=jax.ShapeDtypeStruct((dim, rows), F32),
        grid_spec=pltpu.PrefetchScalarGridSpec(
            num_scalar_prefetch=1,
            grid=(rows // LOOK_TILE,),
            in_specs=[whole(n_chunk, CHUNK, 1), whole(n_micro, micro, 1), whole(tokens, dim), whole(n_micro, micro, dim), pl.BlockSpec((tokens, LOOK_TILE), lambda i, s: (0, i))],
            out_specs=pl.BlockSpec((dim, LOOK_TILE), lambda i, s: (0, i)),
            scratch_shapes=[pltpu.VMEM((dim, tokens), BF16), pltpu.VMEM((n_chunk, dim, CHUNK), BF16)],
        ),
        compiler_params=params(1),
        name="table",
    )(starts, ids_cols, rank_cols, normed, gx, grad)


def solution(mesh):
    def body(token_ids, label_ids, emb_rows, w_in, w_out):
        stage = lax.axis_index("stage")
        n_micro, micro = token_ids.shape
        rows, dim = emb_rows.shape
        tokens = n_micro * micro
        scale = dim ** -0.5
        row_start = stage * rows
        table_t = emb_rows.T
        w1 = w_in[0]
        w2 = w_out[0].T

        flat = token_ids.reshape(-1)
        order_key = flat * tokens + jnp.arange(tokens, dtype=jnp.int32)
        rank = jnp.sum((order_key[None, :] < order_key[:, None]).astype(jnp.int32), axis=1)
        sorted_ids = jnp.sort(order_key) // tokens
        edges = row_start + jnp.arange(rows // LOOK_TILE + 1, dtype=jnp.int32) * LOOK_TILE
        starts = jnp.sum((flat[None, :] < edges[:, None]).astype(jnp.int32), axis=1)
        starts = jnp.concatenate([starts, row_start[None]]).astype(jnp.int32)
        rank_cols = rank.reshape(n_micro, micro, 1)
        ids_rows = sorted_ids.reshape(-1, 1, CHUNK)
        ids_cols = sorted_ids.reshape(-1, CHUNK, 1)

        part = run_lookup(starts, ids_rows, rank_cols, table_t)
        saved, last = run_forward(part, w1, w2)

        labels = (label_ids - row_start).reshape(tokens, 1)
        prob, normed, tile_max, tile_sum, tile_pick = run_head(last.reshape(tokens, dim), labels, table_t, scale)
        top = jnp.max(tile_max, axis=1)
        total = jnp.sum(tile_sum * jnp.exp(tile_max - top[:, None]), axis=1)
        stats = lax.all_gather(jnp.stack([top, total, jnp.sum(tile_pick, axis=1)]), "stage")
        row_max = jnp.max(stats[:, 0], axis=0)
        row_sum = jnp.sum(stats[:, 1] * jnp.exp(stats[:, 0] - row_max), axis=0)
        picked = jnp.sum(stats[:, 2], axis=0)
        loss = jnp.sum(jnp.log(row_sum) + row_max - picked) / tokens
        coef = jnp.exp(tile_max - row_max[:, None]) / row_sum[:, None] * scale
        lab_coef = (jnp.exp(picked - row_max) / row_sum - 1.0) * scale
        grad, grad_n = run_head_grad(prob, coef, labels, lab_coef[:, None], table_t)

        dy, gx, hid, dpre = run_backward(grad_n.reshape(n_micro, micro, dim), last, saved, w1, w2)
        flatten = lambda arr: arr.reshape(tokens, arr.shape[-1])
        grad_first, grad_second = run_weights(flatten(saved), flatten(dpre), flatten(dy), flatten(hid))
        grad_table = run_table(starts, ids_cols, rank_cols, normed, gx, grad)
        return loss.reshape(1), grad_first[None], grad_second.T[None], grad_table.T

    return jax.shard_map(
        body,
        mesh=mesh,
        in_specs=(P("dp", None), P("dp", None), P("stage", None), P("stage", None, None), P("stage", None, None)),
        out_specs=(P("dp"), P(("dp", "stage"), None, None), P(("dp", "stage"), None, None), P(("dp", "stage"), None)),
        check_vma=False,
    )
```

time: 1750 us -> 601 us (0.34)
  matrix products: 730 us -> 0 us
  Pallas kernels: 0 us -> 564 us
  waiting for transfers between devices: 311 us -> 0 us
  local copies, waits for them, and re-layouts: 290 us -> 7.2 us
  other arithmetic: 188 us -> 16.9 us
  starting transfers between devices: 103 us -> 0 us
  blocking collectives: 95.3 us -> 5.42 us
    dot_general x72 -> x0, matrix products: 730 us -> none  [the longest x8 269 us: head_step(): jnp.einsum('tv,td->vd', grad_logits, normed_mb, preferred_element_type=jn...]
    pallas_call x0 -> x7, Pallas kernels: none -> 564 us  [the longest x1 107 us: run_forward(): pl.pallas_call(fwd_kernel, out_shape=(jax.ShapeDtypeStruct(shape, BF16),...]
    psum x11 -> x0, waiting for transfers between devices: 192 us -> none  [the longest x1 79.1 us: stage_body(): lax.psum(jnp.where(is_last, normed_f.astype(jnp.bfloat16), 0), 'stage')]
    ppermute x22 -> x0, waiting for transfers between devices: 119 us -> none  [the longest x11 119 us: bwd_tick(): lax.ppermute(grad_in, 'stage', bwd_pairs)]
    ppermute x22 -> x0, starting transfers between devices: 103 us -> none  [the longest x11 88.6 us: fwd_tick(): return (lax.ppermute(act_out, 'stage', fwd_pairs), saved_in, last_out)]
    unnamed x21 -> x7, local copies, waits for them, and re-layouts: 89.4 us -> 2.07 us
    reduce_sum x18 -> x5, other arithmetic: 66.5 us -> 5.78 us  [the longest x1 2.17 us: body(): total = jnp.sum(tile_sum * jnp.exp(tile_max - top[:, None]), axis=1)]
    while x2 -> x0, local copies, waits for them, and re-layouts: 54 us -> none  [the longest x1 47.6 us: stage_body(): lax.scan(head_step, head_init, (normed, local_lab))]
  transfers between devices with their start and end apart: 33 -> 0, of which waited for: 15 -> 0; matrix products, arithmetic and copies ran while one was open for 22% -> 0% of each run, Pallas kernels for 0% -> 0%
where the time goes in v1:
time: 601 us; the launch traced here: 596 us
  Pallas kernels  564 us (94%)
  other arithmetic  16.9 us (3%)
  local copies, waits for them, and re-layouts  7.2 us (1%)
    pallas_call x1, Pallas kernels, run_forward(): pl.pallas_call(fwd_kernel, out_shape=(jax.ShapeDtypeStruct(shape, BF16),...  107 us
    pallas_call x1, Pallas kernels, run_backward(): pl.pallas_call(bwd_kernel, out_shape=(jax.ShapeDtypeStruct(shape, BF16),...  104 us
    pallas_call x1, Pallas kernels, run_head_grad(): pl.pallas_call(head_grad_kernel, out_shape=(jax.ShapeDtypeStruct((tokens,...  103 us
    pallas_call x1, Pallas kernels, run_head(): pl.pallas_call(functools.partial(head_kernel, scale), out_shape=(jax.Shap...  98.7 us
    pallas_call x1, Pallas kernels, run_table(): pl.pallas_call(table_kernel, out_shape=jax.ShapeDtypeStruct((dim, rows),...  86.9 us
    pallas_call x1, Pallas kernels, run_lookup(): pl.pallas_call(lookup_kernel, out_shape=jax.ShapeDtypeStruct((n_micro, to...  35.7 us
    pallas_call x1, Pallas kernels, run_weights(): pl.pallas_call(weight_kernel, out_shape=(jax.ShapeDtypeStruct((dim, ffn),...  29.6 us

profile of v1, /device:TPU:0, one launch (start us, length us, event | category | flops | bytes accessed | tf_op | source)
XLA Modules:
  0.0 596.4 jit_solution(16413836165643435829)
XLA Ops:
  0.6 0.7 copy.33
  1.3 0.2 convert_reduce_fusion.1
  1.6 0.6 pad_add_fusion.starts
  2.1 5.0 sort.15
  7.2 0.6 add_select_fusion
  7.8 1.8 convert_reduce_fusion
  9.6 1.9 reshape.119.rank_ref
  11.4 35.7 %lookup.1.part = bf16[8,256,960]{2,1,0:T(8,128)(2,1)} custom-call(s32[26]{0:T(128)} %pad_add_fusion.starts, s32[8,1,256]{2,1,0:T(1,128)} %bitcast.61, s32[8,256,1]{2,1,0:T(8,128)} %reshape.119.rank_ref, bf16[960,12288]{1,0:T(8,128)(2,1)} %bitcast.44), custom_call_target="tpu_custom_call" | custom-call | tf_op jit(solution)/shard_map/lookup/pallas_call | solution.py:91
  47.1 106.7 %forward.1 = (bf16[8,256,960]{2,1,0:T(8,128)(2,1)}, bf16[8,256,960]{2,1,0:T(8,128)(2,1)}) custom-call(bf16[8,256,960]{2,1,0:T(8,128)(2,1)} %lookup.1.part, bf16[960,2560]{1,0:T(8,128)(2,1)} %bitcast.48, bf16[960,2560]{1,0:T(8,128)(2,1)} %bitcast.50), custom_call_target="tpu_custom_call" | custom-call | tf_op jit(solution)/shard_map/forward/pallas_call | solution.py:243
  153.9 1.3 copy.35
  155.2 98.7 %head.1 = (bf16[2048,12288]{1,0:T(8,128)(2,1)}, bf16[2048,960]{1,0:T(8,128)(2,1)}, f32[2048,128]{1,0:T(8,128)}, f32[2048,128]{1,0:T(8,128)}, f32[2048,128]{1,0:T(8,128)}) custom-call(bf16[2048,960]{1,0:T(8,128)(2,1)} %bitcast.53, s32[2048,1]{1,0:T(8,128)} %bitcast.56, bf16[960,12288]{1,0:T(8,128)(2,1)} %bitcast.45), custom_call_target="tpu_custom_call" | custom-call | tf_op jit(solution)/shard_map/head/pallas_call | solution.py:281
  254.0 1.6 reduce_sum.66
  255.6 1.6 reduce_max.18
  257.1 2.2 multiply_reduce_fusion
  259.3 5.4 all-gather.1
  264.8 0.1 fusion.5
  264.9 0.6 add_multiply_fusion
  266.2 2.5 divide_multiply_fusion.coef_ref
  268.7 1.4 copy.28.lab_coef_ref
  270.1 102.9 %head_grad.1 = (bf16[2048,12288]{1,0:T(8,128)(2,1)}, f32[2048,960]{1,0:T(8,128)}) custom-call(bf16[2048,12288]{1,0:T(8,128)(2,1)} %get-tuple-element.27.prob_ref, f32[2048,128]{1,0:T(8,128)} %divide_multiply_fusion.coef_ref, s32[2048,1]{1,0:T(8,128)} %bitcast.57, f32[2048,1]{1,0:T(8,128)} %copy.28.lab_coef_ref, bf16[960,12288]{1,0:T(8,128)(2,1)} %bitcast.46), custom_call_target="tpu_custom_call" | custom-call | tf_op jit(solution)/shard_map/head_grad/pallas_call | solution.py:319
  373.0 103.9 %backward.1 = (bf16[8,256,960]{2,1,0:T(8,128)(2,1)}, bf16[8,256,960]{2,1,0:T(8,128)(2,1)}, bf16[8,256,2560]{2,1,0:T(8,128)(2,1)}, bf16[8,256,2560]{2,1,0:T(8,128)(2,1)}) custom-call(f32[8,256,960]{2,1,0:T(8,128)} %bitcast.58, bf16[8,256,960]{2,1,0:T(8,128)(2,1)} %get-tuple-element.22.last, bf16[8,256,960]{2,1,0:T(8,128)(2,1)} %get-tuple-element.26.saved, ...), custom_call_target="tpu_custom_call" | custom-call | tf_op jit(solution)/shard_map/backward/pallas_call | solution.py:485
  476.9 29.6 %weights.1 = (f32[960,2560]{1,0:T(8,128)}, f32[960,2560]{1,0:T(8,128)}) custom-call(bf16[2048,960]{1,0:T(8,128)(2,1)} %bitcast.52, bf16[2048,2560]{1,0:T(8,128)(2,1)} %bitcast.55, bf16[2048,960]{1,0:T(8,128)(2,1)} %bitcast.59, bf16[2048,2560]{1,0:T(8,128)(2,1)} %bitcast.54), custom_call_target="tpu_custom_call" | custom-call | tf_op jit(solution)/shard_map/weights/pallas_call | solution.py:515
  506.5 1.9 reshape.121.ids_ref
  508.4 86.9 %table.1 = f32[960,12288]{1,0:T(8,128)} custom-call(s32[26]{0:T(128)} %pad_add_fusion.starts, s32[8,256,1]{2,1,0:T(8,128)} %reshape.121.ids_ref, s32[8,256,1]{2,1,0:T(8,128)} %reshape.119.rank_ref, bf16[2048,960]{1,0:T(8,128)(2,1)} %get-tuple-element.34.norm_ref, bf16[8,256,960]{2,1,0:T(8,128)(2,1)} %get-tuple-element.35.gx_ref, ...), custom_call_target="tpu_custom_call" | custom-call | tf_op jit(solution)/shard_map/table/pallas_call | solution.py:564
  (11 shorter events, 0.1 us)
Async XLA Ops:
  47.1 106.7 %copy-start.1 = (s32[8,256]{1,0:T(8,128)S(1)}, s32[8,256]{1,0:T(8,128)}, u32[]{:S(2)}) copy-start(s32[8,256]{1,0:T(8,128)} %param.6) | copy-start | bytes 24580
  476.9 29.6 %copy-start = (s32[2048]{0:T(1024)S(1)}, s32[2048]{0:T(1024)}, u32[]{:S(2)}) copy-start(s32[2048]{0:T(1024)} %add_select_fusion) | copy-start | bytes 24580
